TPU v7x, 32 devices: a whole 2x2x4 slice. The times are simulated.
32 devices in a mesh: grp: 4 (over y, x), dev: 8 (over z, core).
Axes of the slice: x: 2, y: 2, z: 4, core: 2. Of those that a mesh axis runs over, the one named last changes fastest.
Arguments:
- acts: bfloat16 [8192, 12288], P(('grp', 'dev')), may hold values from -6 to 6
- grads_out: bfloat16 [8192, 64], P(('grp', 'dev')), may hold values from -0.375 to 0.375
- residual_in: float32 [32, 64, 12288], P(('grp', 'dev')), may hold values from -6 to 6
- sel_index: int32 [32, 64], P(('grp', 'dev')), may hold values from 0 to 6143, as said below
- sel_count: int32 [32], P(('grp', 'dev')), may hold values from 16 to 64, as said below
- momentum_in: float32 [64, 12288], P(None, 'dev'), may hold values from -6 to 6
Outputs:
- residual_out: float32 [32, 64, 12288], P(('grp', 'dev'))
- momentum_out: float32 [64, 12288], P(None, 'dev')
Inputs may be any that keep to these rules, and one draw needn't show every extreme that they name: `sel_index`: the 64 numbers of a row are distinct. `sel_count`: equal to 64 on some device in every draw.
All inputs are finite; a program needn't handle non-finite values.
Results may differ from a plain program's by a relative error of at most 0.0003.
Values sent between devices are 32-bit elements; how exact they have to be, the bound alone decides.
A program may use at most 64 MiB of HBM per device.

v0:
```python
import jax
import jax.numpy as jnp
from jax import lax
from jax.sharding import PartitionSpec as P

momentum_decay = 0.9


def from_behind(block, axis, distance):
    devices = range(lax.axis_size(axis))
    route = [((i - distance) % len(devices), i) for i in devices]
    return lax.ppermute(block, axis, route)


def local(acts, grads_out, residual_in, sel_index, sel_count, momentum_in):
    width = acts.shape[1]
    columns = grads_out.shape[1]
    slots = sel_index.shape[1]
    n_blocks = columns * width // 128
    part_width = momentum_in.shape[1]
    local_grad = lax.dot_general(
        grads_out, acts, (((0,), (0,)), ((), ())), preferred_element_type=jnp.float32
    )
    summed = residual_in[0] + local_grad
    blocks = summed.reshape(n_blocks, 128)
    chosen = sel_index[0]
    valid_rows = (jnp.arange(slots, dtype=jnp.int32) < sel_count[0]).astype(jnp.float32)
    picked = blocks[chosen] * valid_rows[:, None]
    marked = jnp.zeros((n_blocks,), jnp.float32).at[chosen].max(valid_rows)
    kept = (blocks * (1.0 - marked)[:, None]).reshape(1, columns, width)
    labels = chosen.astype(jnp.float32)
    group_vals, group_labels = (
        lax.all_gather(picked, "dev", axis=0, tiled=True),
        lax.all_gather(labels, "dev", axis=0, tiled=True),
    )
    n_groups = lax.axis_size("grp")
    here = lax.axis_index("grp")
    store_vals = jnp.zeros((n_groups,) + group_vals.shape, jnp.float32)
    store_labels = jnp.zeros((n_groups,) + group_labels.shape, jnp.float32)
    store_vals = lax.dynamic_update_index_in_dim(store_vals, group_vals, here, 0)
    store_labels = lax.dynamic_update_index_in_dim(store_labels, group_labels, here, 0)

    def advance(rounds, carry):
        moving_vals, moving_labels, kept_vals, kept_labels = carry
        moving_vals, moving_labels = from_behind((moving_vals, moving_labels), "grp", 1)
        source = (here - rounds) % n_groups
        kept_vals = lax.dynamic_update_index_in_dim(kept_vals, moving_vals, source, 0)
        kept_labels = lax.dynamic_update_index_in_dim(kept_labels, moving_labels, source, 0)
        return (moving_vals, moving_labels, kept_vals, kept_labels)

    carried = lax.fori_loop(
        1, n_groups, advance, (group_vals, group_labels, store_vals, store_labels)
    )
    all_vals = carried[2].reshape(-1, 128)
    all_labels = carried[3].reshape(-1).astype(jnp.int32)
    spread = (
        jnp.zeros((n_blocks, 128), jnp.float32).at[all_labels].add(all_vals).reshape(columns, width)
    )
    total = lax.dynamic_slice_in_dim(spread, lax.axis_index("dev") * part_width, part_width, 1)
    momentum_out = momentum_decay * momentum_in + total
    return (kept, momentum_out)


def solution(mesh):
    placed = (
        P(("grp", "dev"), None),
        P(("grp", "dev"), None),
        P(("grp", "dev"), None, None),
        P(("grp", "dev"), None),
        P(("grp", "dev")),
        P(None, "dev"),
    )
    return jax.shard_map(
        local,
        mesh=mesh,
        in_specs=placed,
        out_specs=(P(("grp", "dev"), None, None), P(None, "dev")),
        check_vma=False,
    )
```

profile of v0, /device:TPU:0, one launch (start us, length us, event | category | flops | bytes accessed | tf_op | source)
XLA Modules:
  0.0 100.5 jit_solution(11768598687038377532)
XLA Ops:
  0.7 0.7 copy-done
  1.4 4.9 %convolution_add_fusion = f32[64,12288]{1,0:T(8,128)S(1)} fusion(bf16[256,64]{0,1:T(8,128)(2,1)S(1)} %copy-done, bf16[256,12288]{1,0:T(8,128)(2,1)} %param.8, f32[1,64,12288]{2,1,0:T(8,128)} %param.10), kind=kOutput, calls=%fused_computation.4 | convolution fusion | flops 403439616 | bytes 12615680 | tf_op jit(solution)/shard_map/dot_general | solution.py:21
  6.3 1.9 %reshape.79 = f32[6144,128]{1,0:T(8,128)} reshape(f32[64,12288]{1,0:T(8,128)S(1)} %convolution_add_fusion) | data formatting | bytes 6291456 | tf_op jit(solution)/shard_map/reshape | solution.py:25
  8.3 2.5 %gather_fusion = f32[64,128]{1,0:T(8,128)S(1)} fusion(f32[6144,128]{1,0:T(8,128)} %reshape.79, s32[1024]{0:T(1024)S(1)} %pad_clamp_fusion), kind=kCustom, calls=%fused_computation | custom fusion | bytes 65792 | tf_op jit(solution)/shard_map/gather | solution.py:28
  11.5 15.9 %all_gather.6 = f32[512,128]{1,0:T(8,128)S(1)} all-gather(f32[64,128]{1,0:T(8,128)S(1)} %broadcast_multiply_fusion), channel_id=1, replica_groups=mesh['grp'=4,'dev'=8] {'dev'}, dimensions={0}, use_global_device_ids=true | all-gather | bytes 294912 | tf_op jit(solution)/shard_map/all_gather | solution.py:33
  27.5 0.6 copy-done.1
  28.1 1.0 copy-done.2
  29.1 0.6 dynamic-slice
  30.4 0.1 bitcast_dynamic-update-slice_fusion.2
  30.5 16.9 %all-reduce = f32[512]{0:T(512)S(1)} all-reduce(f32[512]{0:T(512)S(1)} %bitcast_dynamic-update-slice_fusion.2), channel_id=2, replica_groups=mesh['grp'=4,'dev'=8] {'dev'}, use_global_device_ids=true, to_apply=%add | all-reduce | flops 512 | bytes 4096 | tf_op jit(solution)/shard_map/all_gather | solution.py:34
  47.4 27.6 %while.21 = (s32[]{:T(128)}, f32[512,128]{1,0:T(8,128)}, f32[512]{0:T(512)S(1)}, f32[4,512,128]{2,1,0:T(8,128)}, f32[4,512]{1,0:T(4,128)S(1)}, /*index=5*/s32[]{:T(128)}, s32[]{:T(128)}, s32[]{:T(128)}, s32[]{:T(128)}, s32[]{:T(128)}) while((s32[]{:T(128)}, f32[512,128]{1,0:T(8,128)}, f32[512]{0:T(512)S(1)}, f32[4,512,128]{2,1,0:T(8,128)}, ...), condition=%wide.region_2.3_spmd, body=%wide.region_1.2_spmd.sunk | while | flops 17 | bytes 2113880 | solution.py:51
  47.4 1.5 %collective-permute-start = (f32[512,128]{1,0:T(8,128)}, f32[512,128]{1,0:T(8,128)S(1)}, u32[]{:S(2)}, u32[]{:S(2)}) collective-permute-start(f32[512,128]{1,0:T(8,128)} %get-tuple-element.220), channel_id=1, source_target_pairs={{24,0},{0,8},{8,16},{16,24},{25,1},{1,9},{9,17},{17,25},{26,2},{2,... | collective-permute-start | bytes 786440 | tf_op jit(solution)/shard_map/while/body/eval_jaxpr/ppermute | solution.py:12
  49.0 1.5 %collective-permute-start.1 = (f32[512]{0:T(512)S(1)}, f32[512]{0:T(512)S(1)}, u32[]{:S(2)}, u32[]{:S(2)}) collective-permute-start(f32[512]{0:T(512)S(1)} %get-tuple-element.221), channel_id=1, source_target_pairs={{24,0},{0,8},{8,16},{16,24},{25,1},{1,9},{9,17},{17,25},{26,2},{2,... | collective-permute-start | bytes 6152 | tf_op jit(solution)/shard_map/while/body/eval_jaxpr/ppermute | solution.py:12
  50.5 4.5 %collective-permute-done.1 = f32[512]{0:T(512)S(1)} collective-permute-done((f32[512]{0:T(512)S(1)}, f32[512]{0:T(512)S(1)}, u32[]{:S(2)}, u32[]{:S(2)}) %collective-permute-start.1) | collective-permute-done | bytes 2080 | tf_op jit(solution)/shard_map/while/body/eval_jaxpr/ppermute | solution.py:12
  55.1 0.7 copy.27
  55.8 0.7 bitcast_dynamic-update-slice_fusion.4
  56.5 0.9 collective-permute-start
  57.4 2.0 %collective-permute-start.1 = (f32[512]{0:T(512)S(1)}, f32[512]{0:T(512)S(1)}, u32[]{:S(2)}, u32[]{:S(2)}) collective-permute-start(f32[512]{0:T(512)S(1)} %get-tuple-element.221), channel_id=1, source_target_pairs={{24,0},{0,8},{8,16},{16,24},{25,1},{1,9},{9,17},{17,25},{26,2},{2,... | collective-permute-start | bytes 6152 | tf_op jit(solution)/shard_map/while/body/eval_jaxpr/ppermute | solution.py:12
  59.5 5.1 %collective-permute-done.1 = f32[512]{0:T(512)S(1)} collective-permute-done((f32[512]{0:T(512)S(1)}, f32[512]{0:T(512)S(1)}, u32[]{:S(2)}, u32[]{:S(2)}) %collective-permute-start.1) | collective-permute-done | bytes 2080 | tf_op jit(solution)/shard_map/while/body/eval_jaxpr/ppermute | solution.py:12
  64.6 0.7 copy.27
  65.3 0.7 bitcast_dynamic-update-slice_fusion.4
  66.1 0.7 collective-permute-start
  66.7 2.3 %collective-permute-start.1 = (f32[512]{0:T(512)S(1)}, f32[512]{0:T(512)S(1)}, u32[]{:S(2)}, u32[]{:S(2)}) collective-permute-start(f32[512]{0:T(512)S(1)} %get-tuple-element.221), channel_id=1, source_target_pairs={{24,0},{0,8},{8,16},{16,24},{25,1},{1,9},{9,17},{17,25},{26,2},{2,... | collective-permute-start | bytes 6152 | tf_op jit(solution)/shard_map/while/body/eval_jaxpr/ppermute | solution.py:12
  69.0 4.5 %collective-permute-done.1 = f32[512]{0:T(512)S(1)} collective-permute-done((f32[512]{0:T(512)S(1)}, f32[512]{0:T(512)S(1)}, u32[]{:S(2)}, u32[]{:S(2)}) %collective-permute-start.1) | collective-permute-done | bytes 2080 | tf_op jit(solution)/shard_map/while/body/eval_jaxpr/ppermute | solution.py:12
  73.6 0.7 copy.27
  74.3 0.7 bitcast_dynamic-update-slice_fusion.4
  75.1 13.6 %scatter_custom_fusion.1 = f32[6144,128]{1,0:T(8,128)} fusion(s32[2048]{0:T(1024)S(1)} %bitcast.41, f32[2048,128]{1,0:T(8,128)} %bitcast.38, f32[]{:T(128)} %constant.79.clone.1), kind=kCustom, calls=%fused_computation.7 | custom fusion | flops 262144 | bytes 3146240 | tf_op jit(solution)/shard_map/scatter-add | solution.py:57
  88.7 4.3 %reshape.81 = f32[64,12288]{1,0:T(8,128)} reshape(f32[6144,128]{1,0:T(8,128)} %scatter_custom_fusion.1) | data formatting | bytes 6291456 | tf_op jit(solution)/shard_map/reshape | solution.py:57
  93.0 1.9 %dynamic-slice_add_fusion = f32[64,1536]{1,0:T(8,128)} fusion(f32[64,12288]{1,0:T(8,128)} %reshape.81, s32[]{:T(128)S(6)} %select_n.64, f32[64,1536]{1,0:T(8,128)} %param.13), kind=kLoop, calls=%fused_computation.9 | loop fusion | flops 196608 | bytes 1179652 | tf_op jit(solution)/shard_map/add | solution.py:60
  94.9 0.9 scatter_custom_fusion
  96.0 0.9 mul.34
  96.8 3.6 %fusion = f32[1,64,12288]{2,1,0:T(8,128)} fusion(f32[64,12288]{1,0:T(8,128)S(1)} %convolution_add_fusion, f32[8,8,96,128]{3,2,1,0:T(8,128)S(1)} %bitcast.37), kind=kLoop, calls=%fused_computation.6 | loop fusion | flops 786432 | bytes 9437184 | tf_op jit(solution)/shard_map/mul | solution.py:30
  (30 shorter events, 0.5 us)
Async XLA Ops:
  0.6 0.8 copy-start
  6.3 1.9 %copy-start.3 = (s32[1,64]{1,0:T(1,128)S(1)}, s32[1,64]{1,0:T(1,128)}, u32[]{:S(2)}) copy-start(s32[1,64]{1,0:T(1,128)} %param.11) | copy-start | bytes 772
  6.3 22.8 %copy-start.4 = (u32[32]{0:T(128)S(1)}, u32[32]{0:T(128)}, u32[]{:S(2)}) copy-start(u32[32]{0:T(128)} %constant.93) | copy-start | bytes 388
  27.4 0.7 copy-start.1
  28.1 1.0 copy-start.2
  47.4 7.6 %collective-permute-start = (f32[512,128]{1,0:T(8,128)}, f32[512,128]{1,0:T(8,128)S(1)}, u32[]{:S(2)}, u32[]{:S(2)}) collective-permute-start(f32[512,128]{1,0:T(8,128)} %get-tuple-element.220), channel_id=1, source_target_pairs={{24,0},{0,8},{8,16},{16,24},{25,1},{1,9},{9,17},{17,25},{26,2},{2,... | collective-permute-start | bytes 786440 | tf_op jit(solution)/shard_map/while/body/eval_jaxpr/ppermute | solution.py:12
  49.0 6.0 %collective-permute-start.1 = (f32[512]{0:T(512)S(1)}, f32[512]{0:T(512)S(1)}, u32[]{:S(2)}, u32[]{:S(2)}) collective-permute-start(f32[512]{0:T(512)S(1)} %get-tuple-element.221), channel_id=1, source_target_pairs={{24,0},{0,8},{8,16},{16,24},{25,1},{1,9},{9,17},{17,25},{26,2},{2,... | collective-permute-start | bytes 6152 | tf_op jit(solution)/shard_map/while/body/eval_jaxpr/ppermute | solution.py:12
  56.5 8.1 %collective-permute-start = (f32[512,128]{1,0:T(8,128)}, f32[512,128]{1,0:T(8,128)S(1)}, u32[]{:S(2)}, u32[]{:S(2)}) collective-permute-start(f32[512,128]{1,0:T(8,128)} %get-tuple-element.220), channel_id=1, source_target_pairs={{24,0},{0,8},{8,16},{16,24},{25,1},{1,9},{9,17},{17,25},{26,2},{2,... | collective-permute-start | bytes 786440 | tf_op jit(solution)/shard_map/while/body/eval_jaxpr/ppermute | solution.py:12
  57.4 7.2 %collective-permute-start.1 = (f32[512]{0:T(512)S(1)}, f32[512]{0:T(512)S(1)}, u32[]{:S(2)}, u32[]{:S(2)}) collective-permute-start(f32[512]{0:T(512)S(1)} %get-tuple-element.221), channel_id=1, source_target_pairs={{24,0},{0,8},{8,16},{16,24},{25,1},{1,9},{9,17},{17,25},{26,2},{2,... | collective-permute-start | bytes 6152 | tf_op jit(solution)/shard_map/while/body/eval_jaxpr/ppermute | solution.py:12
  66.1 7.6 %collective-permute-start = (f32[512,128]{1,0:T(8,128)}, f32[512,128]{1,0:T(8,128)S(1)}, u32[]{:S(2)}, u32[]{:S(2)}) collective-permute-start(f32[512,128]{1,0:T(8,128)} %get-tuple-element.220), channel_id=1, source_target_pairs={{24,0},{0,8},{8,16},{16,24},{25,1},{1,9},{9,17},{17,25},{26,2},{2,... | collective-permute-start | bytes 786440 | tf_op jit(solution)/shard_map/while/body/eval_jaxpr/ppermute | solution.py:12
  66.7 6.8 %collective-permute-start.1 = (f32[512]{0:T(512)S(1)}, f32[512]{0:T(512)S(1)}, u32[]{:S(2)}, u32[]{:S(2)}) collective-permute-start(f32[512]{0:T(512)S(1)} %get-tuple-element.221), channel_id=1, source_target_pairs={{24,0},{0,8},{8,16},{16,24},{25,1},{1,9},{9,17},{17,25},{26,2},{2,... | collective-permute-start | bytes 6152 | tf_op jit(solution)/shard_map/while/body/eval_jaxpr/ppermute | solution.py:12
where the time goes:
time: 101 us; the launch traced here: 100 us
  blocking collectives  32.8 us (32%)
  other arithmetic  20.3 us (20%)
  local copies, waits for them, and re-layouts  17.1 us (17%)
  waiting for transfers between devices  14.2 us (14%)
  starting transfers between devices  8.97 us (9%)
  matrix products  4.91 us (5%)
  between operations  2.04 us (2%)
    all_gather x1, blocking collectives, local(): lax.all_gather(labels, 'dev', axis=0, tiled=True)  16.9 us
    all_gather x1, blocking collectives, local(): lax.all_gather(picked, 'dev', axis=0, tiled=True)  15.9 us
    ppermute x6, waiting for transfers between devices, from_behind(): return lax.ppermute(block, axis, route)  14.2 us
    scatter-add x1, other arithmetic, local(): jnp.zeros((n_blocks, 128), jnp.float32).at[all_labels].add(all_vals)  13.6 us
    ppermute x6, starting transfers between devices, from_behind(): return lax.ppermute(block, axis, route)  8.97 us
    dot_general x1, matrix products, local(): lax.dot_general(grads_out, acts, (((0,), (0,)), ((), ())), preferred_elem...  4.91 us
    reshape x1, local copies, waits for them, and re-layouts, local(): jnp.zeros((n_blocks, 128), jnp.float32).at[all_labels].add(all_vals)  4.3 us
    mul x1, other arithmetic, local(): kept = (blocks * (1.0 - marked)[:, None]).reshape(1, columns, width)  3.64 us
  transfers between devices with their start and end apart: 6, of which 3 were waited for; matrix products, arithmetic and copies ran while one was open for 0% of the time, Pallas kernels for 0%

commit v1 on v0

v1 whole, which is shorter than its diff:
```python
import functools

import jax
import jax.numpy as jnp
from jax import lax
from jax.experimental import pallas as pl
from jax.experimental.pallas import tpu as pltpu
from jax.sharding import PartitionSpec as P

momentum_decay = 0.9
LANES = 128
MESH = pl.DeviceIdType.MESH


def tiles_of(width):
    for count in (8, 6, 4, 3, 2):
        if width % (count * 2 * LANES) == 0:
            return count
    return 1


def local_kernel(
    tiles, acts, residual, grads, sel_row, sel_smem, count_smem,
    kept, packed,
    acts_buf, res_buf, summed, kept_buf, in_sem, out_sem,
):
    columns, width = residual.shape[1:]
    slots = sel_row.shape[1]
    blocks_wide = width // LANES
    span = width // tiles
    per_tile = span // LANES

    def fetch(t):
        cols = pl.ds(t * span, span)
        return (
            pltpu.make_async_copy(acts.at[:, cols], acts_buf.at[:, cols], in_sem.at[0, t]),
            pltpu.make_async_copy(residual.at[0, :, cols], res_buf.at[:, cols], in_sem.at[1, t]),
        )

    def put(t):
        cols = pl.ds(t * span, span)
        return pltpu.make_async_copy(kept_buf.at[:, cols], kept.at[0, :, cols], out_sem.at[t])

    for t in range(tiles):
        for copy in fetch(t):
            copy.start()

    number = sel_row[...].astype(jnp.float32)
    row = jnp.floor((number + 0.5) * (1.0 / blocks_wide))
    col = number - row * blocks_wide
    used = lax.broadcasted_iota(jnp.int32, (1, slots), 1) < count_smem[0]
    row_hit = lax.broadcasted_iota(jnp.int32, (columns, slots), 0).astype(jnp.float32) == row
    col_hit = lax.broadcasted_iota(jnp.int32, (blocks_wide, slots), 0).astype(jnp.float32) == col
    taken = lax.dot_general(
        jnp.where(row_hit & used, 1.0, 0.0).astype(jnp.bfloat16),
        jnp.where(col_hit, 1.0, 0.0).astype(jnp.bfloat16),
        (((1,), (1,)), ((), ())),
        preferred_element_type=jnp.float32,
    )
    label = jnp.where(used, col * columns + row, -1.0)
    packed[pl.ds(slots, 8), pl.ds(0, slots)] = jnp.broadcast_to(label, (8, slots))
    if slots < LANES:
        packed[pl.ds(slots, 8), pl.ds(slots, LANES - slots)] = jnp.full(
            (8, LANES - slots), -1.0, jnp.float32
        )

    turned = grads[...].T
    for t in range(tiles):
        for copy in fetch(t):
            copy.wait()
        cols = pl.ds(t * span, span)
        total = res_buf[:, cols] + jnp.dot(
            turned, acts_buf[:, cols], preferred_element_type=jnp.float32
        )
        for j in range(per_tile):
            c = t * per_tile + j
            piece = total[:, j * LANES : (j + 1) * LANES]
            summed[c] = piece
            kept_buf[:, pl.ds(c * LANES, LANES)] = jnp.where(taken[:, c : c + 1] > 0.5, 0.0, piece)
        put(t).start()

    for s in range(slots):
        b = sel_smem[0, s]
        r = lax.div(b, blocks_wide)
        c = b - r * blocks_wide
        packed[pl.ds(s, 1), :] = summed[c, pl.ds(r, 1), :]

    for t in range(tiles):
        put(t).wait()


def gather_kernel(
    sizes, packed, momentum_in, momentum_out, store, total, send_sem, recv_sem
):
    rows_a, rows_b, depth, cores = sizes
    slots = packed.shape[0] - 8
    columns, part_width = momentum_in.shape
    part_blocks = part_width // LANES
    g = lax.axis_index("grp")
    d = lax.axis_index("dev")
    a, b = g // rows_b, g % rows_b
    z, core = d // cores, d % cores

    def group(i, j):
        return lax.rem(a + i, rows_a) * rows_b + lax.rem(b + j, rows_b)

    def member(k, q):
        return lax.rem(z + k, depth) * cores + lax.rem(core + q, cores)

    peers = (
        [(g, member(k, 0)) for k in range(1, depth)]
        + [(g, member(0, q)) for q in range(1, cores)]
        + [(group(i, 0), d) for i in range(1, rows_a)]
        + [(group(0, j), d) for j in range(1, rows_b)]
    )
    barrier = pltpu.get_barrier_semaphore()
    for peer in peers:
        pl.semaphore_signal(barrier, inc=1, device_id=peer, device_id_type=MESH)
    store[g, d] = packed[...]
    pl.semaphore_wait(barrier, len(peers))

    sends = []

    def copy_to(source, slot, peer, index):
        return pltpu.make_async_remote_copy(
            src_ref=source,
            dst_ref=store.at[slot[0], slot[1]],
            send_sem=send_sem.at[index],
            recv_sem=recv_sem.at[slot[0], slot[1]],
            device_id=peer,
            device_id_type=MESH,
        )

    def send(slot, peer, own=False):
        source = packed if own else store.at[slot[0], slot[1]]
        copy = copy_to(source, slot, peer, len(sends))
        sends.append(copy)
        copy.start()

    def arrived(slot):
        copy_to(store.at[slot[0], slot[1]], slot, (g, member(0, 1)), 0).wait_recv()

    def to_partner(slot, own=False):
        for q in range(1, cores):
            send(slot, (g, member(0, q)), own)

    def spread(k, own=False):
        slot = (g, member(k, 0))
        for i in range(1, rows_a):
            send(slot, (group(i, 0), d), own)
        for j in range(1, rows_b):
            send(slot, (group(0, j), d), own)
        to_partner(slot, own)

    base = (d * (part_blocks * columns)).astype(jnp.float32)
    place = lax.broadcasted_iota(jnp.int32, (part_blocks * columns, 1), 0).astype(jnp.float32)
    started = []

    def add(i, j, q):
        blocks = [(group(i, j), member(k, q)) for k in range(depth)]
        vals = jnp.concatenate([store[x, y, :slots, :] for x, y in blocks], axis=0)
        labels = jnp.concatenate(
            [store[x, y, pl.ds(slots, 1), pl.ds(0, slots)] for x, y in blocks], axis=1
        )
        high = vals.astype(jnp.bfloat16)
        low = (vals - high.astype(jnp.float32)).astype(jnp.bfloat16)
        both = jnp.concatenate([high, low], axis=1)
        hit = jnp.where(place == labels - base, 1.0, 0.0).astype(jnp.bfloat16)
        part = jnp.dot(hit, both, preferred_element_type=jnp.float32)
        if started:
            total[...] += part
        else:
            total[...] = part
            started.append(True)

    def add_others(i, j):
        for q in range(1, cores):
            for k in range(depth):
                arrived((group(i, j), member(k, q)))
            add(i, j, q)

    for k in range(1, depth):
        send((g, d), (g, member(depth - k, 0)), True)
    spread(0, True)
    order = sorted(range(1, depth), key=lambda k: min(k, depth - k))
    hops = [(k, i, j) for k in range(depth) for i, j in (
        [(0, j) for j in range(1, rows_b)] if k % 2 == 0 else [(i, 0) for i in range(1, rows_a)]
    )]

    def relay(k, i, j):
        slot = (group(i, j), member(k, 0))
        arrived(slot)
        if j:
            for n in range(1, rows_a):
                send(slot, (group(n, 0), d))
        else:
            for n in range(1, rows_b):
                send(slot, (group(0, n), d))
        to_partner(slot)

    for k in order:
        arrived((g, member(k, 0)))
        spread(k)
    for k, i, j in hops:
        if k == 0:
            relay(k, i, j)
    add(0, 0, 0)
    for k, i, j in hops:
        if k:
            relay(k, i, j)
    add_others(0, 0)
    for i in range(rows_a):
        for j in range(rows_b):
            if i == 0 and j == 0:
                continue
            for k in range(depth):
                relayed = (k, i, j) in hops
                if not relayed:
                    slot = (group(i, j), member(k, 0))
                    arrived(slot)
                    to_partner(slot)
            add(i, j, 0)
            if (i, j) != (rows_a - 1, rows_b - 1) or True:
                add_others(i, j)

    for c in range(part_blocks):
        rows = pl.ds(c * columns, columns)
        cols = pl.ds(c * LANES, LANES)
        momentum_out[:, cols] = momentum_decay * momentum_in[:, cols] + (
            total[rows, pl.ds(0, LANES)] + total[rows, pl.ds(LANES, LANES)]
        )
    for copy in sends:
        copy.wait_send()


def local(mesh_sizes, acts, grads_out, residual_in, sel_index, sel_count, momentum_in):
    groups, members = mesh_sizes
    tokens, width = acts.shape
    columns = grads_out.shape[1]
    slots = sel_index.shape[1]
    part_width = momentum_in.shape[1]
    tiles = tiles_of(width)
    vmem = pl.BlockSpec(memory_space=pltpu.VMEM)
    smem = pl.BlockSpec(memory_space=pltpu.SMEM)
    hbm = pl.BlockSpec(memory_space=pl.ANY)
    kept, packed = pl.pallas_call(
        functools.partial(local_kernel, tiles),
        out_shape=(
            jax.ShapeDtypeStruct(residual_in.shape, jnp.float32),
            jax.ShapeDtypeStruct((slots + 8, LANES), jnp.float32),
        ),
        in_specs=[hbm, hbm, vmem, vmem, smem, smem],
        out_specs=(hbm, vmem),
        scratch_shapes=[
            pltpu.VMEM((tokens, width), jnp.bfloat16),
            pltpu.VMEM((columns, width), jnp.float32),
            pltpu.VMEM((width // LANES, columns, LANES), jnp.float32),
            pltpu.VMEM((columns, width), jnp.float32),
            pltpu.SemaphoreType.DMA((2, tiles)),
            pltpu.SemaphoreType.DMA((tiles,)),
        ],
        name="select",
    )(acts, residual_in, grads_out, sel_index, sel_index, sel_count)

    rows_b = max(n for n in range(1, groups + 1) if groups % n == 0 and n * n <= groups)
    cores = 2 if members % 2 == 0 else 1
    sizes = (groups // rows_b, rows_b, members // cores, cores)
    rows_a, rows_b, depth, cores = sizes
    n_sends = (
        depth - 1 + depth * (rows_a * rows_b - 1) + depth * groups * (cores - 1)
    )
    momentum_out = pl.pallas_call(
        functools.partial(gather_kernel, sizes),
        out_shape=jax.ShapeDtypeStruct(momentum_in.shape, jnp.float32),
        in_specs=[vmem, vmem],
        out_specs=vmem,
        scratch_shapes=[
            pltpu.VMEM((groups, members, slots + 8, LANES), jnp.float32),
            pltpu.VMEM((columns * part_width // LANES, 2 * LANES), jnp.float32),
            pltpu.SemaphoreType.DMA((n_sends,)),
            pltpu.SemaphoreType.DMA((groups, members)),
        ],
        compiler_params=pltpu.CompilerParams(collective_id=0, has_side_effects=True),
        name="gather",
    )(packed, momentum_in)
    return (kept, momentum_out)


def solution(mesh):
    placed = (
        P(("grp", "dev"), None),
        P(("grp", "dev"), None),
        P(("grp", "dev"), None, None),
        P(("grp", "dev"), None),
        P(("grp", "dev")),
        P(None, "dev"),
    )
    return jax.shard_map(
        functools.partial(local, (mesh.shape["grp"], mesh.shape["dev"])),
        mesh=mesh,
        in_specs=placed,
        out_specs=(P(("grp", "dev"), None, None), P(None, "dev")),
        check_vma=False,
    )
```

time: 101 us -> 32 us (0.32)
  blocking collectives: 32.8 us -> 0 us
  Pallas kernels: 0 us -> 26.9 us
  other arithmetic: 20.3 us -> 0 us
  waiting for transfers between devices: 14.2 us -> 0 us
  local copies, waits for them, and re-layouts: 17.1 us -> 3.26 us
  starting transfers between devices: 8.97 us -> 0 us
  matrix products: 4.91 us -> 0 us
    all_gather x2 -> x0, blocking collectives: 32.8 us -> none  [the longest x1 16.9 us: local(): lax.all_gather(labels, 'dev', axis=0, tiled=True)]
    pallas_call x0 -> x2, Pallas kernels: none -> 26.9 us  [the longest x1 19.8 us: local(): pl.pallas_call(functools.partial(gather_kernel, sizes), out_shape=jax.Sha...]
    ppermute x6 -> x0, waiting for transfers between devices: 14.2 us -> none  [from_behind(): return lax.ppermute(block, axis, route)]
    scatter-add x1 -> x0, other arithmetic: 13.6 us -> none  [local(): jnp.zeros((n_blocks, 128), jnp.float32).at[all_labels].add(all_vals)]
    ppermute x6 -> x0, starting transfers between devices: 8.97 us -> none  [from_behind(): return lax.ppermute(block, axis, route)]
    reshape x2 -> x0, local copies, waits for them, and re-layouts: 6.21 us -> none  [the longest x1 4.3 us: local(): jnp.zeros((n_blocks, 128), jnp.float32).at[all_labels].add(all_vals)]
    dot_general x1 -> x0, matrix products: 4.91 us -> none  [local(): lax.dot_general(grads_out, acts, (((0,), (0,)), ((), ())), preferred_elem...]
    mul x2 -> x0, other arithmetic: 3.72 us -> none  [the longest x1 3.64 us: local(): kept = (blocks * (1.0 - marked)[:, None]).reshape(1, columns, width)]
  transfers between devices with their start and end apart: 6 -> 0, of which waited for: 3 -> 0; matrix products, arithmetic and copies ran while one was open for 0% -> 0% of each run, Pallas kernels for 0% -> 0%
where the time goes in v1:
time: 32 us; the launch traced here: 31.4 us
  Pallas kernels  26.9 us (84%)
  local copies, waits for them, and re-layouts  3.26 us (10%)
  between operations  1.29 us (4%)
    pallas_call x1, Pallas kernels, local(): pl.pallas_call(functools.partial(gather_kernel, sizes), out_shape=jax.Sha...  19.8 us
    pallas_call x1, Pallas kernels, local(): pl.pallas_call(functools.partial(local_kernel, tiles), out_shape=(jax.Sha...  7.1 us
    unnamed x2, local copies, waits for them, and re-layouts  3.26 us

profile of v1, /device:TPU:0, one launch (start us, length us, event | category | flops | bytes accessed | tf_op | source)
XLA Modules:
  0.0 31.4 jit_solution(13413654090576920897)
XLA Ops:
  1.3 1.5 %copy.8.grads = bf16[256,64]{1,0:T(8,128)(2,1)} copy(bf16[256,64]{0,1:T(8,128)(2,1)} %param.7) | data formatting | bytes 65536 | tf_op args[1]
  2.8 7.1 %select.1 = (f32[1,64,12288]{2,1,0:T(8,128)}, f32[72,128]{1,0:T(8,128)}) custom-call(bf16[256,12288]{1,0:T(8,128)(2,1)} %acts.1, f32[1,64,12288]{2,1,0:T(8,128)} %residual.1, bf16[256,64]{1,0:T(8,128)(2,1)} %copy.8.grads, s32[1,64]{1,0:T(1,128)} %sel_smem.1, s32[1,64]{1,0:T(1,128)} %sel_smem.1, s32[1]{0:T(128)S(6)} %copy.10.count_smem), custom_call_target="tpu_custom_call" | custom-call | tf_op jit(solution)/shard_map/select/pallas_call | solution.py:246
  9.9 19.8 %gather.1 = f32[64,1536]{1,0:T(8,128)} custom-call(f32[72,128]{1,0:T(8,128)} %get-tuple-element.5.packed, f32[64,1536]{1,0:T(8,128)} %momentum_in.1), custom_call_target="tpu_custom_call" | custom-call | tf_op jit(solution)/shard_map/gather/pallas_call | solution.py:272
  29.7 1.8 %copy.11 = f32[64,1536]{1,0:T(8,128)} copy(f32[64,1536]{1,0:T(8,128)} %gather.1) | data formatting | bytes 786432

commit v2 on v1

--- a/solution.py
+++ b/solution.py
@@ -19,10 +19,10 @@
     return 1
 
 
-def local_kernel(
-    tiles, acts, residual, grads, sel_row, sel_smem, count_smem,
-    kept, packed,
-    acts_buf, res_buf, summed, kept_buf, in_sem, out_sem,
+def gather_kernel(
+    tiles, sizes, acts, residual, grads_in, sel_in, sel_smem, count_smem, momentum_hbm,
+    kept, momentum_out,
+    grads, sel_row, momentum_in, small_sem, acts_buf, res_buf, summed, packed, store, total, in_sem, send_sem, recv_sem,
 ):
     columns, width = residual.shape[1:]
     slots = sel_row.shape[1]
@@ -37,26 +37,47 @@
             pltpu.make_async_copy(residual.at[0, :, cols], res_buf.at[:, cols], in_sem.at[1, t]),
         )
 
-    def put(t):
-        cols = pl.ds(t * span, span)
-        return pltpu.make_async_copy(kept_buf.at[:, cols], kept.at[0, :, cols], out_sem.at[t])
-
+    small = [
+        pltpu.make_async_copy(sel_in, sel_row, small_sem.at[0]),
+        pltpu.make_async_copy(grads_in, grads, small_sem.at[1]),
+        pltpu.make_async_copy(momentum_hbm, momentum_in, small_sem.at[2]),
+    ]
+    for copy in small[:2]:
+        copy.start()
     for t in range(tiles):
         for copy in fetch(t):
             copy.start()
-
+    small[2].start()
+
+    rows_a, rows_b, depth, cores = sizes
+    part_width = momentum_in.shape[1]
+    part_blocks = part_width // LANES
+    g = lax.axis_index("grp")
+    d = lax.axis_index("dev")
+    a, b = g // rows_b, g % rows_b
+    z, core = d // cores, d % cores
+
+    def group(i, j):
+        return lax.rem(a + i, rows_a) * rows_b + lax.rem(b + j, rows_b)
+
+    def member(k, q):
+        return lax.rem(z + k, depth) * cores + lax.rem(core + q, cores)
+
+    peers = (
+        [(g, member(k, 0)) for k in range(1, depth)]
+        + [(g, member(0, q)) for q in range(1, cores)]
+        + [(group(i, 0), d) for i in range(1, rows_a)]
+        + [(group(0, j), d) for j in range(1, rows_b)]
+    )
+    barrier = pltpu.get_barrier_semaphore()
+    for peer in peers:
+        pl.semaphore_signal(barrier, inc=1, device_id=peer, device_id_type=MESH)
+
+    small[0].wait()
     number = sel_row[...].astype(jnp.float32)
     row = jnp.floor((number + 0.5) * (1.0 / blocks_wide))
     col = number - row * blocks_wide
     used = lax.broadcasted_iota(jnp.int32, (1, slots), 1) < count_smem[0]
-    row_hit = lax.broadcasted_iota(jnp.int32, (columns, slots), 0).astype(jnp.float32) == row
-    col_hit = lax.broadcasted_iota(jnp.int32, (blocks_wide, slots), 0).astype(jnp.float32) == col
-    taken = lax.dot_general(
-        jnp.where(row_hit & used, 1.0, 0.0).astype(jnp.bfloat16),
-        jnp.where(col_hit, 1.0, 0.0).astype(jnp.bfloat16),
-        (((1,), (1,)), ((), ())),
-        preferred_element_type=jnp.float32,
-    )
     label = jnp.where(used, col * columns + row, -1.0)
     packed[pl.ds(slots, 8), pl.ds(0, slots)] = jnp.broadcast_to(label, (8, slots))
     if slots < LANES:
@@ -64,58 +85,21 @@
             (8, LANES - slots), -1.0, jnp.float32
         )
 
-    turned = grads[...].T
+    small[1].wait()
+    turned = grads[...]
     for t in range(tiles):
         for copy in fetch(t):
             copy.wait()
         cols = pl.ds(t * span, span)
-        total = res_buf[:, cols] + jnp.dot(
+        sums = res_buf[:, cols] + jnp.dot(
             turned, acts_buf[:, cols], preferred_element_type=jnp.float32
         )
         for j in range(per_tile):
-            c = t * per_tile + j
-            piece = total[:, j * LANES : (j + 1) * LANES]
-            summed[c] = piece
-            kept_buf[:, pl.ds(c * LANES, LANES)] = jnp.where(taken[:, c : c + 1] > 0.5, 0.0, piece)
-        put(t).start()
-
+            summed[t * per_tile + j] = sums[:, j * LANES : (j + 1) * LANES]
     for s in range(slots):
-        b = sel_smem[0, s]
-        r = lax.div(b, blocks_wide)
-        c = b - r * blocks_wide
-        packed[pl.ds(s, 1), :] = summed[c, pl.ds(r, 1), :]
-
-    for t in range(tiles):
-        put(t).wait()
-
-
-def gather_kernel(
-    sizes, packed, momentum_in, momentum_out, store, total, send_sem, recv_sem
-):
-    rows_a, rows_b, depth, cores = sizes
-    slots = packed.shape[0] - 8
-    columns, part_width = momentum_in.shape
-    part_blocks = part_width // LANES
-    g = lax.axis_index("grp")
-    d = lax.axis_index("dev")
-    a, b = g // rows_b, g % rows_b
-    z, core = d // cores, d % cores
-
-    def group(i, j):
-        return lax.rem(a + i, rows_a) * rows_b + lax.rem(b + j, rows_b)
-
-    def member(k, q):
-        return lax.rem(z + k, depth) * cores + lax.rem(core + q, cores)
-
-    peers = (
-        [(g, member(k, 0)) for k in range(1, depth)]
-        + [(g, member(0, q)) for q in range(1, cores)]
-        + [(group(i, 0), d) for i in range(1, rows_a)]
-        + [(group(0, j), d) for j in range(1, rows_b)]
-    )
-    barrier = pltpu.get_barrier_semaphore()
-    for peer in peers:
-        pl.semaphore_signal(barrier, inc=1, device_id=peer, device_id_type=MESH)
+        block = sel_smem[0, s]
+        r = lax.div(block, blocks_wide)
+        packed[pl.ds(s, 1), :] = summed[block - r * blocks_wide, pl.ds(r, 1), :]
     store[g, d] = packed[...]
     pl.semaphore_wait(barrier, len(peers))
 
@@ -182,6 +166,22 @@
     for k in range(1, depth):
         send((g, d), (g, member(depth - k, 0)), True)
     spread(0, True)
+
+    row_hit = lax.broadcasted_iota(jnp.int32, (columns, slots), 0).astype(jnp.float32) == row
+    col_hit = lax.broadcasted_iota(jnp.int32, (blocks_wide, slots), 0).astype(jnp.float32) == col
+    taken = lax.dot_general(
+        jnp.where(row_hit & used, 1.0, 0.0).astype(jnp.bfloat16),
+        jnp.where(col_hit, 1.0, 0.0).astype(jnp.bfloat16),
+        (((1,), (1,)), ((), ())),
+        preferred_element_type=jnp.float32,
+    )
+
+    def keep(first, last):
+        for c in range(first, last):
+            kept[0, :, pl.ds(c * LANES, LANES)] = jnp.where(
+                taken[:, c : c + 1] > 0.5, 0.0, summed[c]
+            )
+
     order = sorted(range(1, depth), key=lambda k: min(k, depth - k))
     hops = [(k, i, j) for k in range(depth) for i, j in (
         [(0, j) for j in range(1, rows_b)] if k % 2 == 0 else [(i, 0) for i in range(1, rows_a)]
@@ -198,7 +198,8 @@
                 send(slot, (group(0, n), d))
         to_partner(slot)
 
-    for k in order:
+    for n, k in enumerate(order):
+        keep(blocks_wide * n // len(order), blocks_wide * (n + 1) // len(order))
         arrived((g, member(k, 0)))
         spread(k)
     for k, i, j in hops:
@@ -220,9 +221,9 @@
                     arrived(slot)
                     to_partner(slot)
             add(i, j, 0)
-            if (i, j) != (rows_a - 1, rows_b - 1) or True:
-                add_others(i, j)
-
+            add_others(i, j)
+
+    small[2].wait()
     for c in range(part_blocks):
         rows = pl.ds(c * columns, columns)
         cols = pl.ds(c * LANES, LANES)
@@ -231,6 +232,17 @@
         )
     for copy in sends:
         copy.wait_send()
+
+
+def finish_kernel(kept_in, momentum_in, kept, momentum, sem):
+    copies = (
+        pltpu.make_async_copy(momentum_in, momentum, sem.at[0]),
+        pltpu.make_async_copy(kept_in, kept, sem.at[1]),
+    )
+    for copy in copies:
+        copy.start()
+    for copy in copies:
+        copy.wait()
 
 
 def local(mesh_sizes, acts, grads_out, residual_in, sel_index, sel_count, momentum_in):
@@ -242,48 +254,52 @@
     tiles = tiles_of(width)
     vmem = pl.BlockSpec(memory_space=pltpu.VMEM)
     smem = pl.BlockSpec(memory_space=pltpu.SMEM)
-    hbm = pl.BlockSpec(memory_space=pl.ANY)
-    kept, packed = pl.pallas_call(
-        functools.partial(local_kernel, tiles),
+    hbm = pl.BlockSpec(memory_space=pltpu.HBM)
+    rows_b = max(n for n in range(1, groups + 1) if groups % n == 0 and n * n <= groups)
+    cores = 2 if members % 2 == 0 else 1
+    rows_a, depth = groups // rows_b, members // cores
+    sizes = (rows_a, rows_b, depth, cores)
+    n_sends = depth - 1 + depth * (groups - 1) + depth * groups * (cores - 1)
+    kept, momentum_out = pl.pallas_call(
+        functools.partial(gather_kernel, tiles, sizes),
         out_shape=(
-            jax.ShapeDtypeStruct(residual_in.shape, jnp.float32),
-            jax.ShapeDtypeStruct((slots + 8, LANES), jnp.float32),
+            pltpu.VMEM(residual_in.shape, jnp.float32),
+            pltpu.VMEM(momentum_in.shape, jnp.float32),
         ),
-        in_specs=[hbm, hbm, vmem, vmem, smem, smem],
-        out_specs=(hbm, vmem),
+        in_specs=[hbm, hbm, hbm, hbm, smem, smem, hbm],
+        out_specs=(vmem, vmem),
         scratch_shapes=[
+            pltpu.VMEM((columns, tokens), jnp.bfloat16),
+            pltpu.VMEM((1, slots), jnp.int32),
+            pltpu.VMEM(momentum_in.shape, jnp.float32),
+            pltpu.SemaphoreType.DMA((3,)),
             pltpu.VMEM((tokens, width), jnp.bfloat16),
             pltpu.VMEM((columns, width), jnp.float32),
             pltpu.VMEM((width // LANES, columns, LANES), jnp.float32),
-            pltpu.VMEM((columns, width), jnp.float32),
-            pltpu.SemaphoreType.DMA((2, tiles)),
-            pltpu.SemaphoreType.DMA((tiles,)),
-        ],
-        name="select",
-    )(acts, residual_in, grads_out, sel_index, sel_index, sel_count)
-
-    rows_b = max(n for n in range(1, groups + 1) if groups % n == 0 and n * n <= groups)
-    cores = 2 if members % 2 == 0 else 1
-    sizes = (groups // rows_b, rows_b, members // cores, cores)
-    rows_a, rows_b, depth, cores = sizes
-    n_sends = (
-        depth - 1 + depth * (rows_a * rows_b - 1) + depth * groups * (cores - 1)
-    )
-    momentum_out = pl.pallas_call(
-        functools.partial(gather_kernel, sizes),
-        out_shape=jax.ShapeDtypeStruct(momentum_in.shape, jnp.float32),
-        in_specs=[vmem, vmem],
-        out_specs=vmem,
-        scratch_shapes=[
+            pltpu.VMEM((slots + 8, LANES), jnp.float32),
             pltpu.VMEM((groups, members, slots + 8, LANES), jnp.float32),
             pltpu.VMEM((columns * part_width // LANES, 2 * LANES), jnp.float32),
+            pltpu.SemaphoreType.DMA((2, tiles)),
             pltpu.SemaphoreType.DMA((n_sends,)),
             pltpu.SemaphoreType.DMA((groups, members)),
         ],
-        compiler_params=pltpu.CompilerParams(collective_id=0, has_side_effects=True),
+        compiler_params=pltpu.CompilerParams(
+            collective_id=0, has_side_effects=True, vmem_limit_bytes=40 << 20
+        ),
         name="gather",
-    )(packed, momentum_in)
-    return (kept, momentum_out)
+    )(acts, residual_in, grads_out.T, sel_index, sel_index, sel_count, momentum_in)
+    return pl.pallas_call(
+        finish_kernel,
+        out_shape=(
+            jax.ShapeDtypeStruct(residual_in.shape, jnp.float32),
+            jax.ShapeDtypeStruct(momentum_in.shape, jnp.float32),
+        ),
+        in_specs=[vmem, vmem],
+        out_specs=(hbm, hbm),
+        scratch_shapes=[pltpu.SemaphoreType.DMA((2,))],
+        compiler_params=pltpu.CompilerParams(vmem_limit_bytes=8 << 20),
+        name="finish",
+    )(kept, momentum_out)
 
 
 def solution(mesh):

time: 32 us -> 32.3 us (level)
  the two profiles are of different devices: /device:TPU:0 before, /device:TPU:1 now
where the time goes in v2:
time: 32.3 us; the launch traced here: 32 us
  Pallas kernels  23.6 us (73%)
  local copies, waits for them, and re-layouts  7.07 us (22%)
  between operations  1.3 us (4%)
    pallas_call x1, Pallas kernels, local(): pl.pallas_call(functools.partial(gather_kernel, tiles, sizes), out_shape=...  21.8 us
    unnamed x10, local copies, waits for them, and re-layouts  7.07 us
    pallas_call x1, Pallas kernels, local(): pl.pallas_call(finish_kernel, out_shape=(jax.ShapeDtypeStruct(residual_in...  1.81 us

profile of v2, /device:TPU:1, one launch (start us, length us, event | category | flops | bytes accessed | tf_op | source)
XLA Modules:
  0.0 32.0 jit_solution(9835489237991335164)
XLA Ops:
  1.3 0.0 copy-start
  1.3 2.8 %copy-done = bf16[256,12288]{1,0:T(8,128)(2,1)S(1)} copy-done((bf16[256,12288]{1,0:T(8,128)(2,1)S(1)}, bf16[256,12288]{1,0:T(8,128)(2,1)}, u32[]{:S(2)}) %copy-start) | copy-done | bytes 6291480
  4.1 0.0 copy-start.1
  4.1 1.9 %copy-done.1 = f32[1,64,12288]{2,1,0:T(8,128)S(1)} copy-done((f32[1,64,12288]{2,1,0:T(8,128)S(1)}, f32[1,64,12288]{2,1,0:T(8,128)}, u32[]{:S(2)}) %copy-start.1) | copy-done | bytes 3145752
  6.0 0.0 copy-start.2
  6.0 1.0 %copy-done.2 = f32[64,1536]{1,0:T(8,128)S(1)} copy-done((f32[64,1536]{1,0:T(8,128)S(1)}, f32[64,1536]{1,0:T(8,128)}, u32[]{:S(2)}) %copy-start.2) | copy-done | bytes 393240
  6.9 0.0 copy-start.3
  7.0 0.8 %copy-done.3 = bf16[256,64]{0,1:T(8,128)(2,1)S(1)} copy-done((bf16[256,64]{0,1:T(8,128)(2,1)S(1)}, bf16[256,64]{0,1:T(8,128)(2,1)}, u32[]{:S(2)}) %copy-start.3) | copy-done | bytes 32792
  7.7 0.0 copy-start.4
  7.7 0.7 %copy-done.4 = s32[1,64]{1,0:T(1,128)S(1)} copy-done((s32[1,64]{1,0:T(1,128)S(1)}, s32[1,64]{1,0:T(1,128)}, u32[]{:S(2)}) %copy-start.4) | copy-done | bytes 280
  8.4 21.8 %gather.1 = (f32[1,64,12288]{2,1,0:T(8,128)S(1)}, f32[64,1536]{1,0:T(8,128)S(1)}) custom-call(bf16[256,12288]{1,0:T(8,128)(2,1)S(1)} %copy-done, f32[1,64,12288]{2,1,0:T(8,128)S(1)} %copy-done.1, bf16[64,256]{1,0:T(8,128)(2,1)S(1)} %bitcast.1, s32[1,64]{1,0:T(1,128)S(1)} %copy-done.4, s32[1,64]{1,0:T(1,128)S(1)} %copy-done.4, s32[1]{0:T(128)S(6)} %copy.8.count_smem, ...), custom_call_target="tpu_custom_call" | custom-call | tf_op jit(solution)/shard_map/gather/pallas_call | solution.py:263
  30.2 1.8 %finish.1 = (f32[1,64,12288]{2,1,0:T(8,128)}, f32[64,1536]{1,0:T(8,128)}) custom-call(f32[1,64,12288]{2,1,0:T(8,128)S(1)} %get-tuple-element.4.kept_in, f32[64,1536]{1,0:T(8,128)S(1)} %get-tuple-element.5.momentum_in), custom_call_target="tpu_custom_call" | custom-call | tf_op jit(solution)/shard_map/finish/pallas_call | solution.py:291
Async XLA Ops:
  1.3 2.8 %copy-start = (bf16[256,12288]{1,0:T(8,128)(2,1)S(1)}, bf16[256,12288]{1,0:T(8,128)(2,1)}, u32[]{:S(2)}) copy-start(bf16[256,12288]{1,0:T(8,128)(2,1)} %acts.1) | copy-start | bytes 18874372
  4.1 1.9 %copy-start.1 = (f32[1,64,12288]{2,1,0:T(8,128)S(1)}, f32[1,64,12288]{2,1,0:T(8,128)}, u32[]{:S(2)}) copy-start(f32[1,64,12288]{2,1,0:T(8,128)} %residual.1) | copy-start | bytes 9437188
  6.0 1.0 %copy-start.2 = (f32[64,1536]{1,0:T(8,128)S(1)}, f32[64,1536]{1,0:T(8,128)}, u32[]{:S(2)}) copy-start(f32[64,1536]{1,0:T(8,128)} %momentum_hbm.1) | copy-start | bytes 1179652
  6.9 0.8 %copy-start.3 = (bf16[256,64]{0,1:T(8,128)(2,1)S(1)}, bf16[256,64]{0,1:T(8,128)(2,1)}, u32[]{:S(2)}) copy-start(bf16[256,64]{0,1:T(8,128)(2,1)} %param.7) | copy-start | bytes 98308
  7.7 0.7 %copy-start.4 = (s32[1,64]{1,0:T(1,128)S(1)}, s32[1,64]{1,0:T(1,128)}, u32[]{:S(2)}) copy-start(s32[1,64]{1,0:T(1,128)} %sel_smem.1) | copy-start | bytes 772

commit v3 on v2

--- a/solution.py
+++ b/solution.py
@@ -9,6 +9,7 @@
 
 momentum_decay = 0.9
 LANES = 128
+vmem_bytes = 67043328
 MESH = pl.DeviceIdType.MESH
 
 
@@ -60,14 +61,20 @@
     def group(i, j):
         return lax.rem(a + i, rows_a) * rows_b + lax.rem(b + j, rows_b)
 
+    near = [sorted(range(depth), key=lambda y: (abs(y - x), y)) for x in range(depth)]
+
     def member(k, q):
-        return lax.rem(z + k, depth) * cores + lax.rem(core + q, cores)
+        place = near[0][k]
+        for x in range(1, depth):
+            place = jnp.where(z == x, near[x][k], place)
+        return place * cores + lax.rem(core + q, cores)
 
     peers = (
         [(g, member(k, 0)) for k in range(1, depth)]
         + [(g, member(0, q)) for q in range(1, cores)]
         + [(group(i, 0), d) for i in range(1, rows_a)]
         + [(group(0, j), d) for j in range(1, rows_b)]
+        + [(group(i, j), d) for i in range(1, rows_a) for j in range(1, rows_b) if 0 < depth]
     )
     barrier = pltpu.get_barrier_semaphore()
     for peer in peers:
@@ -134,6 +141,10 @@
             send(slot, (group(i, 0), d), own)
         for j in range(1, rows_b):
             send(slot, (group(0, j), d), own)
+        if k >= 0:
+            for i in range(1, rows_a):
+                for j in range(1, rows_b):
+                    send(slot, (group(i, j), d), own)
         to_partner(slot, own)
 
     base = (d * (part_blocks * columns)).astype(jnp.float32)
@@ -163,8 +174,8 @@
                 arrived((group(i, j), member(k, q)))
             add(i, j, q)
 
-    for k in range(1, depth):
-        send((g, d), (g, member(depth - k, 0)), True)
+    for k in range(depth - 1, 0, -1):
+        send((g, d), (g, member(k, 0)), True)
     spread(0, True)
 
     row_hit = lax.broadcasted_iota(jnp.int32, (columns, slots), 0).astype(jnp.float32) == row
@@ -182,46 +193,63 @@
                 taken[:, c : c + 1] > 0.5, 0.0, summed[c]
             )
 
-    order = sorted(range(1, depth), key=lambda k: min(k, depth - k))
-    hops = [(k, i, j) for k in range(depth) for i, j in (
-        [(0, j) for j in range(1, rows_b)] if k % 2 == 0 else [(i, 0) for i in range(1, rows_a)]
-    )]
-
-    def relay(k, i, j):
-        slot = (group(i, j), member(k, 0))
-        arrived(slot)
-        if j:
-            for n in range(1, rows_a):
-                send(slot, (group(n, 0), d))
-        else:
-            for n in range(1, rows_b):
-                send(slot, (group(0, n), d))
-        to_partner(slot)
-
-    for n, k in enumerate(order):
-        keep(blocks_wide * n // len(order), blocks_wide * (n + 1) // len(order))
+    def relayed(k):
+        if k % 2 == 0:
+            return [(0, j) for j in range(1, rows_b)]
+        return [(i, 0) for i in range(1, rows_a)]
+
+    def straight(k):
+        if k % 2 == 0:
+            return [(i, 0) for i in range(1, rows_a)]
+        return [(0, j) for j in range(1, rows_b)]
+
+    def pass_on(k):
+        for i, j in relayed(k):
+            slot = (group(i, j), member(k, 0))
+            arrived(slot)
+            if k < 0:
+                if j:
+                    for n in range(1, rows_a):
+                        send(slot, (group(n, 0), d))
+                else:
+                    for n in range(1, rows_b):
+                        send(slot, (group(0, n), d))
+            to_partner(slot)
+        for i, j in straight(k):
+            slot = (group(i, j), member(k, 0))
+            arrived(slot)
+            to_partner(slot)
+
+    def pass_far(k):
+        for i in range(1, rows_a):
+            for j in range(1, rows_b):
+                slot = (group(i, j), member(k, 0))
+                arrived(slot)
+                to_partner(slot)
+
+    for k in range(1, depth):
+        keep(blocks_wide * (k - 1) // (depth - 1), blocks_wide * k // (depth - 1))
         arrived((g, member(k, 0)))
         spread(k)
-    for k, i, j in hops:
-        if k == 0:
-            relay(k, i, j)
+        pass_on(k - 1)
     add(0, 0, 0)
-    for k, i, j in hops:
-        if k:
-            relay(k, i, j)
+    for k in range(depth - 1):
+        pass_far(k)
+    pass_on(depth - 1)
     add_others(0, 0)
     for i in range(rows_a):
         for j in range(rows_b):
-            if i == 0 and j == 0:
-                continue
-            for k in range(depth):
-                relayed = (k, i, j) in hops
-                if not relayed:
-                    slot = (group(i, j), member(k, 0))
-                    arrived(slot)
-                    to_partner(slot)
-            add(i, j, 0)
-            add_others(i, j)
+            if (i == 0) != (j == 0):
+                add(i, j, 0)
+    pass_far(depth - 1)
+    for i in range(rows_a):
+        for j in range(rows_b):
+            if i and j:
+                add(i, j, 0)
+    for i in range(rows_a):
+        for j in range(rows_b):
+            if i or j:
+                add_others(i, j)
 
     small[2].wait()
     for c in range(part_blocks):
@@ -260,6 +288,8 @@
     rows_a, depth = groups // rows_b, members // cores
     sizes = (rows_a, rows_b, depth, cores)
     n_sends = depth - 1 + depth * (groups - 1) + depth * groups * (cores - 1)
+    results = 4 * (columns * width + columns * part_width)
+    room = (vmem_bytes - results - (16 << 10)) // 4096 * 4096
     kept, momentum_out = pl.pallas_call(
         functools.partial(gather_kernel, tiles, sizes),
         out_shape=(
@@ -284,7 +314,7 @@
             pltpu.SemaphoreType.DMA((groups, members)),
         ],
         compiler_params=pltpu.CompilerParams(
-            collective_id=0, has_side_effects=True, vmem_limit_bytes=40 << 20
+            collective_id=0, has_side_effects=True, vmem_limit_bytes=room
         ),
         name="gather",
     )(acts, residual_in, grads_out.T, sel_index, sel_index, sel_count, momentum_in)

time: 32.3 us -> 25.4 us (0.79)
  the two profiles are of different devices: /device:TPU:1 before, /device:TPU:0 now
where the time goes in v3:
time: 25.4 us; the launch traced here: 25.2 us
  Pallas kernels  23.9 us (94%)
  between operations  1.29 us (5%)
    pallas_call x1, Pallas kernels, local(): pl.pallas_call(functools.partial(gather_kernel, tiles, sizes), out_shape=...  22.1 us
    pallas_call x1, Pallas kernels, local(): pl.pallas_call(finish_kernel, out_shape=(jax.ShapeDtypeStruct(residual_in...  1.81 us

profile of v3, /device:TPU:0, one launch (start us, length us, event | category | flops | bytes accessed | tf_op | source)
XLA Modules:
  0.0 25.2 jit_solution(1148942186746750405)
XLA Ops:
  1.3 22.1 %gather.1 = (f32[1,64,12288]{2,1,0:T(8,128)S(1)}, f32[64,1536]{1,0:T(8,128)S(1)}) custom-call(bf16[256,12288]{1,0:T(8,128)(2,1)} %acts.1, f32[1,64,12288]{2,1,0:T(8,128)} %residual.1, bf16[64,256]{1,0:T(8,128)(2,1)} %bitcast.1, s32[1,64]{1,0:T(1,128)} %sel_smem.1, s32[1,64]{1,0:T(1,128)} %sel_smem.1, s32[1]{0:T(128)S(6)} %copy.8.count_smem, ...), custom_call_target="tpu_custom_call" | custom-call | tf_op jit(solution)/shard_map/gather/pallas_call | solution.py:293
  23.4 1.8 %finish.1 = (f32[1,64,12288]{2,1,0:T(8,128)}, f32[64,1536]{1,0:T(8,128)}) custom-call(f32[1,64,12288]{2,1,0:T(8,128)S(1)} %get-tuple-element.4.kept_in, f32[64,1536]{1,0:T(8,128)S(1)} %get-tuple-element.5.momentum_in), custom_call_target="tpu_custom_call" | custom-call | tf_op jit(solution)/shard_map/finish/pallas_call | solution.py:321
